TPU v7x, 32 devices: a 4x4x1 block of a 4x4x8 slice. The times are simulated.
32 devices in a mesh: rep: 1 (over z), row: 4 (over y), col: 4 (over x), core: 2 (over core).
Axes of the slice: x: 4, y: 4, z: 1, core: 2. Of those that a mesh axis runs over, the one named last changes fastest.
The devices are a block of a 4x4x8 slice.
Arguments:
- x: bfloat16 [2, 8192, 896], P(None, ('rep', 'row', 'col', 'core'))
- route_idx: int32 [2, 8192, 8], P(None, ('rep', 'row', 'col', 'core'))
- gates: float32 [2, 8192, 8], P(None, ('rep', 'row', 'col', 'core'))
- w_gate: bfloat16 [64, 896, 640], P(('rep', 'row', 'col', 'core'))
- w_up: bfloat16 [64, 896, 640], P(('rep', 'row', 'col', 'core'))
- w_down: bfloat16 [64, 640, 896], P(('rep', 'row', 'col', 'core'))
- grad_y: bfloat16 [2, 8192, 896], P(None, ('rep', 'row', 'col', 'core'))
Outputs:
- output 1: bfloat16 [2, 8192, 896], P(None, ('rep', 'row', 'col', 'core'))
- output 2: bfloat16 [2, 8192, 896], P(None, ('rep', 'row', 'col', 'core'))
- output 3: float32 [2, 8192, 8], P(None, ('rep', 'row', 'col', 'core'))
- output 4: float32 [64, 896, 640], P(('rep', 'row', 'col', 'core'))
- output 5: float32 [64, 896, 640], P(('rep', 'row', 'col', 'core'))
- output 6: float32 [64, 640, 896], P(('rep', 'row', 'col', 'core'))
All inputs are finite; a program needn't handle non-finite values.
Results may differ from a plain program's by a relative error of at most 0.0104298.
Values are sent between devices in bfloat16 or wider.
A program may use at most 768 MiB of HBM per device.

v0:
```python
import jax
import jax.numpy as jnp
from jax import lax
from jax.sharding import PartitionSpec as P

GROUP_AXES = ("row", "col", "core")
ALL_AXES = ("rep", "row", "col", "core")


def route_tables(route_ids, gates, group_size, capacity, local_experts):
    expert_ids = jnp.arange(group_size)[None, :] * local_experts + jnp.arange(local_experts)[:, None]
    expert_hits = route_ids[None, None, :, :] == expert_ids[:, :, None, None]
    member = jnp.sum(expert_hits.astype(jnp.int32), axis=3)
    slot_rank = jnp.cumsum(member, axis=2) - member
    disp_mask = (member[:, :, None, :] > 0) & (slot_rank[:, :, None, :] == jnp.arange(capacity)[None, None, :, None])
    slot_pos = jnp.sum(jnp.where(expert_hits, slot_rank[:, :, :, None], 0), axis=(0, 1))
    slot_addr = (route_ids % local_experts) * (group_size * capacity) + (route_ids // local_experts) * capacity + slot_pos
    row_gate = jnp.zeros((local_experts * group_size * capacity,), jnp.float32).at[slot_addr.reshape(-1)].set(gates.reshape(-1))
    return disp_mask.astype(jnp.bfloat16), slot_addr, row_gate


def expert_forward(x_rows, w_gate, w_up, w_down):
    gate_pre = jnp.einsum("lnd,ldf->lnf", x_rows, w_gate, preferred_element_type=jnp.float32).astype(jnp.bfloat16)
    up_pre = jnp.einsum("lnd,ldf->lnf", x_rows, w_up, preferred_element_type=jnp.float32).astype(jnp.bfloat16)
    gate_f = gate_pre.astype(jnp.float32)
    hidden = (gate_f * jax.nn.sigmoid(gate_f) * up_pre.astype(jnp.float32)).astype(jnp.bfloat16)
    exp_out = jnp.einsum("lnf,lfd->lnd", hidden, w_down, preferred_element_type=jnp.float32).astype(jnp.bfloat16)
    return exp_out, gate_pre, up_pre, hidden


def expert_backward(x_rows, d_out, gate_pre, up_pre, hidden, w_gate, w_up, w_down):
    gate_f = gate_pre.astype(jnp.float32)
    up_f = up_pre.astype(jnp.float32)
    sigmoid_g = jax.nn.sigmoid(gate_f)
    d_act = jnp.einsum("lnd,lfd->lnf", d_out, w_down, preferred_element_type=jnp.float32)
    d_up = (d_act * gate_f * sigmoid_g).astype(jnp.bfloat16)
    d_gate = (d_act * up_f * sigmoid_g * (1.0 + gate_f * (1.0 - sigmoid_g))).astype(jnp.bfloat16)
    g_down = jnp.einsum("lnf,lnd->lfd", hidden, d_out, preferred_element_type=jnp.float32)
    g_gate = jnp.einsum("lnd,lnf->ldf", x_rows, d_gate, preferred_element_type=jnp.float32)
    g_up = jnp.einsum("lnd,lnf->ldf", x_rows, d_up, preferred_element_type=jnp.float32)
    d_in = (jnp.einsum("lnf,ldf->lnd", d_gate, w_gate, preferred_element_type=jnp.float32) + jnp.einsum("lnf,ldf->lnd", d_up, w_up, preferred_element_type=jnp.float32)).astype(jnp.bfloat16)
    return d_in, g_gate, g_up, g_down


def solution(mesh):
    group_size = mesh.shape["row"] * mesh.shape["col"] * mesh.shape["core"]
    tok_spec = P(None, ALL_AXES, None)
    w_spec = P(ALL_AXES, None, None)

    def exchange(send_buf):
        return lax.all_to_all(send_buf, GROUP_AXES, 1, 1, tiled=True)

    def moe_layer(x, route_idx, gates, w_gate, w_up, w_down, grad_y):
        local_experts = w_gate.shape[0]
        tok_dev = x.shape[1]
        model_dim = x.shape[2]
        capacity = tok_dev // 2
        buf_rows = group_size * capacity
        buf_shape = (local_experts, group_size, capacity, model_dim)
        flat_shape = (local_experts * buf_rows, model_dim)
        outs_y, outs_dx, outs_dg = [], [], []
        sum_gate = jnp.zeros(w_gate.shape, jnp.float32)
        sum_up = jnp.zeros(w_up.shape, jnp.float32)
        sum_down = jnp.zeros(w_down.shape, jnp.float32)
        for micro_idx in range(2):
            x_mb = x[micro_idx]
            dy_mb = grad_y[micro_idx]
            gate_mb = gates[micro_idx]
            disp_mask, slot_addr, row_gate = route_tables(route_idx[micro_idx], gate_mb, group_size, capacity, local_experts)
            send_x = jnp.einsum("lgct,td->lgcd", disp_mask, x_mb, preferred_element_type=jnp.float32).astype(jnp.bfloat16)
            x_rows = exchange(send_x).reshape(local_experts, buf_rows, model_dim)
            exp_out, gate_pre, up_pre, hidden = expert_forward(x_rows, w_gate, w_up, w_down)
            out_back = exchange(exp_out.reshape(buf_shape)).reshape(flat_shape)
            out_slots = jnp.take(out_back, slot_addr, axis=0)
            outs_y.append(jnp.sum(gate_mb[:, :, None] * out_slots.astype(jnp.float32), axis=1).astype(jnp.bfloat16))
            outs_dg.append(jnp.einsum("td,tkd->tk", dy_mb, out_slots, preferred_element_type=jnp.float32))
            dy_rows = jnp.einsum("lgct,td->lgcd", disp_mask, dy_mb, preferred_element_type=jnp.float32)
            send_dout = (row_gate.reshape(local_experts, group_size, capacity)[..., None] * dy_rows).astype(jnp.bfloat16)
            d_out = exchange(send_dout).reshape(local_experts, buf_rows, model_dim)
            d_in, g_gate, g_up, g_down = expert_backward(x_rows, d_out, gate_pre, up_pre, hidden, w_gate, w_up, w_down)
            dx_back = exchange(d_in.reshape(buf_shape)).reshape(flat_shape)
            outs_dx.append(jnp.sum(jnp.take(dx_back, slot_addr, axis=0).astype(jnp.float32), axis=1).astype(jnp.bfloat16))
            sum_gate = sum_gate + g_gate
            sum_up = sum_up + g_up
            sum_down = sum_down + g_down
        return (jnp.stack(outs_y), jnp.stack(outs_dx), jnp.stack(outs_dg), sum_gate, sum_up, sum_down)

    return jax.shard_map(moe_layer, mesh=mesh, in_specs=(tok_spec, tok_spec, tok_spec, w_spec, w_spec, w_spec, tok_spec), out_specs=(tok_spec, tok_spec, tok_spec, w_spec, w_spec, w_spec), check_vma=False)
```

profile of v0, /device:TPU:97, one launch (start us, length us, event | category | flops | bytes accessed | tf_op | source)
XLA Modules:
  0.0 1663.2 jit_solution(14971297499672964965)
XLA Ops:
  6.9 8.1 scatter_custom_fusion.1
  15.0 6.0 multiply_convert_fusion
  20.9 7.4 copy.130
  28.3 9.1 all-to-all-start.6
  37.5 4.7 convolution_convert_fusion
  42.2 7.3 copy.112
  49.5 165.5 %all-to-all-done.6 = bf16[2,32,128,896]{3,2,0,1:T(8,128)(2,1)} async-done(((bf16[2,32,128,896]{3,2,0,1:T(8,128)(2,1)}), bf16[2,32,128,896]{3,2,0,1:T(8,128)(2,1)}, u32[]{:S(2)}, u32[]{:S(2)}) %all-to-all-start.6) | async-done | bytes 14680096 | tf_op jit(solution)/shard_map/all_to_all | solution.py:51
  215.0 25.3 %all-to-all-start.2 = ((bf16[2,32,128,896]{3,2,0,1:T(8,128)(2,1)}), bf16[2,32,128,896]{3,2,0,1:T(8,128)(2,1)}, u32[]{:S(2)}, u32[]{:S(2)}) async-start(bf16[2,32,128,896]{3,2,0,1:T(8,128)(2,1)} %copy.112), calls=%async_computation.2 | async-start | bytes 29360128 | tf_op jit(solution)/shard_map/all_to_all | solution.py:51
  240.3 4.7 convolution_convert_fusion.1
  245.0 7.4 copy.103
  252.4 168.4 %all-to-all-done.2 = bf16[2,32,128,896]{3,2,0,1:T(8,128)(2,1)} async-done(((bf16[2,32,128,896]{3,2,0,1:T(8,128)(2,1)}), bf16[2,32,128,896]{3,2,0,1:T(8,128)(2,1)}, u32[]{:S(2)}, u32[]{:S(2)}) %all-to-all-start.2) | async-done | bytes 14680096 | tf_op jit(solution)/shard_map/all_to_all | solution.py:51
  420.8 18.6 %all-to-all-start = ((bf16[2,32,128,896]{3,2,0,1:T(8,128)(2,1)}), bf16[2,32,128,896]{3,2,0,1:T(8,128)(2,1)}, u32[]{:S(2)}, u32[]{:S(2)}) async-start(bf16[2,32,128,896]{3,2,0,1:T(8,128)(2,1)} %copy.103), calls=%async_computation | async-start | bytes 29360128 | tf_op jit(solution)/shard_map/all_to_all | solution.py:51
  440.3 8.1 scatter_custom_fusion
  448.4 5.0 multiply_convert_fusion.1
  453.3 7.4 copy.121
  460.7 155.1 %all-to-all-done = bf16[2,32,128,896]{3,2,0,1:T(8,128)(2,1)} async-done(((bf16[2,32,128,896]{3,2,0,1:T(8,128)(2,1)}), bf16[2,32,128,896]{3,2,0,1:T(8,128)(2,1)}, u32[]{:S(2)}, u32[]{:S(2)}) %all-to-all-start) | async-done | bytes 14680096 | tf_op jit(solution)/shard_map/all_to_all | solution.py:51
  615.9 26.0 %all-to-all-start.4 = ((bf16[2,32,128,896]{3,2,0,1:T(8,128)(2,1)}), bf16[2,32,128,896]{3,2,0,1:T(8,128)(2,1)}, u32[]{:S(2)}, u32[]{:S(2)}) async-start(bf16[2,32,128,896]{3,2,0,1:T(8,128)(2,1)} %copy.121), calls=%async_computation.4 | async-start | bytes 29360128 | tf_op jit(solution)/shard_map/all_to_all | solution.py:51
  647.7 13.7 copy.113
  661.4 18.6 %convolution_convert_fusion.4 = bf16[2,4096,640]{2,1,0:T(8,128)(2,1)} fusion(bf16[2,4096,896]{2,1,0:T(8,128)(2,1)} %bitcast.150, bf16[2,896,640]{2,1,0:T(8,128)(2,1)S(1)} %copy-done.17), kind=kOutput, calls=%fused_computation.50 | convolution fusion | flops 9400483840 | bytes 27459584 | tf_op jit(solution)/shard_map/lnd,ldf->lnf/dot_general | solution.py:24
  680.0 18.6 %convolution_convert_fusion.5 = bf16[2,4096,640]{2,1,0:T(8,128)(2,1)} fusion(bf16[2,4096,896]{2,1,0:T(8,128)(2,1)} %bitcast.151, bf16[2,896,640]{2,1,0:T(8,128)(2,1)S(1)} %copy-done.14), kind=kOutput, calls=%fused_computation.51 | convolution fusion | flops 9400483840 | bytes 27459584 | tf_op jit(solution)/shard_map/lnd,ldf->lnf/dot_general | solution.py:23
  698.6 21.9 %convolution_convert_fusion.2 = bf16[2,4096,896]{2,1,0:T(8,128)(2,1)} fusion(bf16[2,640,896]{2,1,0:T(8,128)(2,1)S(1)} %copy-done, bf16[2,4096,640]{2,1,0:T(8,128)(2,1)} %convolution_convert_fusion.4, bf16[2,4096,640]{2,1,0:T(8,128)(2,1)} %convolution_convert_fusion.5), kind=kOutput, calls=%fused_computation.44 | convolution fusion | flops 9444524032 | bytes 37945344 | tf_op jit(solution)/shard_map/lnf,lfd->lnd/dot_general | solution.py:27
  720.5 13.6 copy.114
  734.1 13.6 copy.104
  747.7 74.6 %all-to-all-done.4 = bf16[2,32,128,896]{3,2,0,1:T(8,128)(2,1)} async-done(((bf16[2,32,128,896]{3,2,0,1:T(8,128)(2,1)}), bf16[2,32,128,896]{3,2,0,1:T(8,128)(2,1)}, u32[]{:S(2)}, u32[]{:S(2)}) %all-to-all-start.4) | async-done | bytes 14680096 | tf_op jit(solution)/shard_map/all_to_all | solution.py:51
  822.2 19.9 %all-to-all-start.3 = ((bf16[2,32,128,896]{3,2,0,1:T(8,128)(2,1)}), bf16[2,32,128,896]{3,2,0,1:T(8,128)(2,1)}, u32[]{:S(2)}, u32[]{:S(2)}) async-start(bf16[2,32,128,896]{3,2,0,1:T(8,128)(2,1)} %copy.114), calls=%async_computation.3 | async-start | bytes 29360128 | tf_op jit(solution)/shard_map/all_to_all | solution.py:51
  842.2 19.0 %convolution_convert_fusion.6 = bf16[2,4096,640]{2,1,0:T(8,128)(2,1)} fusion(bf16[2,4096,896]{2,1,0:T(8,128)(2,1)} %bitcast.156, bf16[2,896,640]{2,1,0:T(8,128)(2,1)} %param.13), kind=kOutput, calls=%fused_computation.52 | convolution fusion | flops 9400483840 | bytes 27459584 | tf_op jit(solution)/shard_map/lnd,ldf->lnf/dot_general | solution.py:24
  861.1 13.8 copy.122
  874.9 18.5 %convolution_convert_fusion.7 = bf16[2,4096,640]{2,1,0:T(8,128)(2,1)} fusion(bf16[2,4096,896]{2,1,0:T(8,128)(2,1)} %bitcast.157, bf16[2,896,640]{2,1,0:T(8,128)(2,1)S(1)} %copy-done.15), kind=kOutput, calls=%fused_computation.53 | convolution fusion | flops 9400483840 | bytes 27459584 | tf_op jit(solution)/shard_map/lnd,ldf->lnf/dot_general | solution.py:23
  893.4 35.9 %fusion.13 = (bf16[2,4096,640]{2,1,0:T(8,128)(2,1)}, bf16[2,4096,640]{2,1,0:T(8,128)(2,1)}, bf16[2,4096,640]{2,1,0:T(8,128)(2,1)}) fusion(bf16[2,4096,640]{2,1,0:T(8,128)(2,1)} %convolution_convert_fusion.7, bf16[2,4096,640]{2,1,0:T(8,128)(2,1)} %convolution_convert_fusion.6, bf16[2,4096,896]{2,1,0:T(8,128)(2,1)} %bitcast.154, ...), kind=kOutput, calls=%fused_computation.35 | convolution fusion | flops 9489612800 | bytes 69402624 | tf_op jit(solution)/shard_map/lnd,lfd->lnf/dot_general | solution.py:35
  929.4 19.4 %convolution_convert_fusion.3 = bf16[2,4096,896]{2,1,0:T(8,128)(2,1)} fusion(bf16[2,4096,640]{2,1,0:T(8,128)(2,1)} %get-tuple-element.17, bf16[2,640,896]{2,1,0:T(8,128)(2,1)S(1)} %copy-done), kind=kOutput, calls=%fused_computation.45 | convolution fusion | flops 9402580992 | bytes 27459584 | tf_op jit(solution)/shard_map/lnf,lfd->lnd/dot_general | solution.py:27
  948.8 13.6 copy.105
  962.4 13.6 copy.131
  976.0 44.5 %all-to-all-done.3 = bf16[2,32,128,896]{3,2,0,1:T(8,128)(2,1)} async-done(((bf16[2,32,128,896]{3,2,0,1:T(8,128)(2,1)}), bf16[2,32,128,896]{3,2,0,1:T(8,128)(2,1)}, u32[]{:S(2)}, u32[]{:S(2)}) %all-to-all-start.3) | async-done | bytes 14680096 | tf_op jit(solution)/shard_map/all_to_all | solution.py:51
  1020.5 21.6 %all-to-all-start.1 = ((bf16[2,32,128,896]{3,2,0,1:T(8,128)(2,1)}), bf16[2,32,128,896]{3,2,0,1:T(8,128)(2,1)}, u32[]{:S(2)}, u32[]{:S(2)}) async-start(bf16[2,32,128,896]{3,2,0,1:T(8,128)(2,1)} %copy.105), calls=%async_computation.1 | async-start | bytes 29360128 | tf_op jit(solution)/shard_map/all_to_all | solution.py:51
  1042.2 27.9 %fusion.19 = (bf16[2,4096,640]{2,1,0:T(8,128)(2,1)}, bf16[2,4096,640]{2,1,0:T(8,128)(2,1)}) fusion(bf16[2,4096,640]{2,1,0:T(8,128)(2,1)} %convolution_convert_fusion.5, bf16[2,4096,640]{2,1,0:T(8,128)(2,1)} %convolution_convert_fusion.4, bf16[2,4096,896]{2,1,0:T(8,128)(2,1)} %bitcast.160, bf16[2,640,896]{2,1,0:T(8,128)(2,1)S(1)} %copy-done), kind=kOutput, calls=%fused_computation.41 | convolution fusion | flops 9473884160 | bytes 58916864 | tf_op jit(solution)/shard_map/lnd,lfd->lnf/dot_general | solution.py:35
  1070.1 22.0 %fusion.87 = f32[2,4096,896]{2,1,0:T(8,128)} fusion(bf16[2,4096,640]{2,1,0:T(8,128)(2,1)} %get-tuple-element.16, bf16[2,896,640]{2,1,0:T(8,128)(2,1)} %param.12), kind=kOutput, calls=%fused_computation.179 | convolution fusion | flops 9395240960 | bytes 42139648 | tf_op jit(solution)/shard_map/lnf,ldf->lnd/dot_general | solution.py:41
  1092.0 24.7 %add_convert_fusion = bf16[2,4096,896]{2,1,0:T(8,128)(2,1)} fusion(f32[2,4096,896]{2,1,0:T(8,128)} %fusion.87, bf16[2,4096,640]{2,1,0:T(8,128)(2,1)} %get-tuple-element.15, bf16[2,896,640]{2,1,0:T(8,128)(2,1)S(1)} %copy-done.18), kind=kOutput, calls=%fused_computation.14 | convolution fusion | flops 9409921024 | bytes 56819712 | tf_op jit(solution)/shard_map/lnf,ldf->lnd/dot_general | solution.py:41
  1116.8 13.6 copy.132
  1130.3 89.4 %all-to-all-done.1 = bf16[2,32,128,896]{3,2,0,1:T(8,128)(2,1)} async-done(((bf16[2,32,128,896]{3,2,0,1:T(8,128)(2,1)}), bf16[2,32,128,896]{3,2,0,1:T(8,128)(2,1)}, u32[]{:S(2)}, u32[]{:S(2)}) %all-to-all-start.1) | async-done | bytes 14680096 | tf_op jit(solution)/shard_map/all_to_all | solution.py:51
  1219.7 24.9 %all-to-all-start.7 = ((bf16[2,32,128,896]{3,2,0,1:T(8,128)(2,1)}), bf16[2,32,128,896]{3,2,0,1:T(8,128)(2,1)}, u32[]{:S(2)}, u32[]{:S(2)}) async-start(bf16[2,32,128,896]{3,2,0,1:T(8,128)(2,1)} %copy.132), calls=%async_computation.7 | async-start | bytes 29360128 | tf_op jit(solution)/shard_map/all_to_all | solution.py:51
  1244.7 20.2 %fusion.86 = f32[2,4096,896]{2,1,0:T(8,128)} fusion(bf16[2,4096,640]{2,1,0:T(8,128)(2,1)} %get-tuple-element.14, bf16[2,896,640]{2,1,0:T(8,128)(2,1)S(1)} %copy-done.16), kind=kOutput, calls=%fused_computation.178 | convolution fusion | flops 9395240960 | bytes 42139648 | tf_op jit(solution)/shard_map/lnf,ldf->lnd/dot_general | solution.py:41
  1264.9 25.4 %add_convert_fusion.1 = bf16[2,4096,896]{2,1,0:T(8,128)(2,1)} fusion(f32[2,4096,896]{2,1,0:T(8,128)} %fusion.86, bf16[2,4096,640]{2,1,0:T(8,128)(2,1)} %get-tuple-element.13, bf16[2,896,640]{2,1,0:T(8,128)(2,1)} %param.13), kind=kOutput, calls=%fused_computation.16 | convolution fusion | flops 9409921024 | bytes 56819712 | tf_op jit(solution)/shard_map/lnf,ldf->lnd/dot_general | solution.py:41
  1290.2 13.6 copy.123
  1303.8 19.1 %fusion.89 = f32[2,896,640]{2,1,0:T(8,128)} fusion(bf16[2,4096,896]{2,1,0:T(8,128)(2,1)} %bitcast.158, bf16[2,4096,640]{2,1,0:T(8,128)(2,1)} %get-tuple-element.13), kind=kOutput, calls=%fused_computation.181 | convolution fusion | flops 9395240960 | bytes 29753344 | tf_op jit(solution)/shard_map/lnd,lnf->ldf/dot_general | solution.py:40
  1323.0 19.0 %fusion.88 = f32[2,896,640]{2,1,0:T(8,128)} fusion(bf16[2,4096,896]{2,1,0:T(8,128)(2,1)} %bitcast.159, bf16[2,4096,640]{2,1,0:T(8,128)(2,1)} %get-tuple-element.14), kind=kOutput, calls=%fused_computation.180 | convolution fusion | flops 9395240960 | bytes 29753344 | tf_op jit(solution)/shard_map/lnd,lnf->ldf/dot_general | solution.py:39
  1342.0 19.0 %convolution_add_fusion.1 = f32[2,896,640]{2,1,0:T(8,128)} fusion(f32[2,896,640]{2,1,0:T(8,128)} %fusion.89, bf16[2,4096,896]{2,1,0:T(8,128)(2,1)} %bitcast.152, bf16[2,4096,640]{2,1,0:T(8,128)(2,1)} %get-tuple-element.15), kind=kOutput, calls=%fused_computation.73 | convolution fusion | flops 9396387840 | bytes 34340864 | tf_op jit(solution)/shard_map/lnd,lnf->ldf/dot_general | solution.py:40
  1361.0 64.0 %all-to-all-done.7 = bf16[2,32,128,896]{3,2,0,1:T(8,128)(2,1)} async-done(((bf16[2,32,128,896]{3,2,0,1:T(8,128)(2,1)}), bf16[2,32,128,896]{3,2,0,1:T(8,128)(2,1)}, u32[]{:S(2)}, u32[]{:S(2)}) %all-to-all-start.7) | async-done | bytes 14680096 | tf_op jit(solution)/shard_map/all_to_all | solution.py:51
  1425.0 19.5 %all-to-all-start.5 = ((bf16[2,32,128,896]{3,2,0,1:T(8,128)(2,1)}), bf16[2,32,128,896]{3,2,0,1:T(8,128)(2,1)}, u32[]{:S(2)}, u32[]{:S(2)}) async-start(bf16[2,32,128,896]{3,2,0,1:T(8,128)(2,1)} %copy.123), calls=%async_computation.5 | async-start | bytes 29360128 | tf_op jit(solution)/shard_map/all_to_all | solution.py:51
  1444.5 18.0 %fusion.90 = f32[2,640,896]{2,1,0:T(8,128)} fusion(bf16[2,4096,640]{2,1,0:T(8,128)(2,1)} %get-tuple-element.17, bf16[2,4096,896]{2,1,0:T(8,128)(2,1)} %bitcast.155), kind=kOutput, calls=%fused_computation.182 | convolution fusion | flops 9395240960 | bytes 29753344 | tf_op jit(solution)/shard_map/lnf,lnd->lfd/dot_general | solution.py:38
  1462.6 18.6 %convolution_add_fusion.2 = f32[2,896,640]{2,1,0:T(8,128)} fusion(f32[2,896,640]{2,1,0:T(8,128)} %fusion.88, bf16[2,4096,896]{2,1,0:T(8,128)(2,1)} %bitcast.153, bf16[2,4096,640]{2,1,0:T(8,128)(2,1)} %get-tuple-element.16), kind=kOutput, calls=%fused_computation.74 | convolution fusion | flops 9396387840 | bytes 34340864 | tf_op jit(solution)/shard_map/lnd,lnf->ldf/dot_general | solution.py:39
  1481.1 20.0 %convolution_add_fusion = f32[2,640,896]{2,1,0:T(8,128)} fusion(f32[2,640,896]{2,1,0:T(8,128)} %fusion.90, bf16[2,4096,896]{2,1,0:T(8,128)(2,1)} %bitcast.161, bf16[2,4096,640]{2,1,0:T(8,128)(2,1)} %convolution_convert_fusion.4, bf16[2,4096,640]{2,1,0:T(8,128)(2,1)} %convolution_convert_fusion.5), kind=kOutput, calls=%fused_computation.72 | convolution fusion | flops 9438330880 | bytes 44826624 | tf_op jit(solution)/shard_map/lnf,lnd->lfd/dot_general | solution.py:38
  1501.2 13.6 copy.115
  1514.7 17.5 %gather_fusion.1 = bf16[2048,896]{1,0:T(8,128)(2,1)} fusion(bf16[8192,896]{1,0:T(8,128)(2,1)} %bitcast.148, s32[2048]{0:T(1024)S(1)} %copy-done.4), kind=kCustom, calls=%fused_computation.1.clone | custom fusion | bytes 7348224 | tf_op jit(solution)/shard_map/jit(_take)/gather | solution.py:74
  1532.3 5.0 fusion.37
  1537.4 14.0 copy.106
  1551.4 17.6 %gather_fusion = bf16[2048,896]{1,0:T(8,128)(2,1)} fusion(bf16[8192,896]{1,0:T(8,128)(2,1)} %bitcast.149, s32[2048]{0:T(1024)S(1)} %copy-done.3), kind=kCustom, calls=%fused_computation.clone | custom fusion | bytes 7348224 | tf_op jit(solution)/shard_map/jit(_take)/gather | solution.py:74
  1569.0 5.0 fusion.36
  1574.0 13.6 copy.133
  1587.6 17.5 %gather_fusion.3 = bf16[2048,896]{1,0:T(8,128)(2,1)} fusion(bf16[8192,896]{1,0:T(8,128)(2,1)} %bitcast.146, s32[2048]{0:T(1024)S(1)} %copy-done.4), kind=kCustom, calls=%fused_computation.3.clone | custom fusion | bytes 7348224 | tf_op jit(solution)/shard_map/jit(_take)/gather | solution.py:82
  1605.1 5.0 fusion.34
  1610.1 4.9 multiply_reduce_fusion
  1618.7 5.4 all-to-all-done.5
  1624.1 13.6 copy.124
  1637.7 17.7 %gather_fusion.2 = bf16[2048,896]{1,0:T(8,128)(2,1)} fusion(bf16[8192,896]{1,0:T(8,128)(2,1)} %bitcast.147, s32[2048]{0:T(1024)S(1)} %copy-done.3), kind=kCustom, calls=%fused_computation.2.clone | custom fusion | bytes 7348224 | tf_op jit(solution)/shard_map/jit(_take)/gather | solution.py:82
  (92 shorter events, 24.1 us)
Async XLA Ops:
  0.6 698.0 %copy-start = (bf16[2,640,896]{2,1,0:T(8,128)(2,1)S(1)}, bf16[2,640,896]{2,1,0:T(8,128)(2,1)}, u32[]{:S(2)}) copy-start(bf16[2,640,896]{2,1,0:T(8,128)(2,1)} %param.14) | copy-start | bytes 6881284
  28.3 9.2 copy-start.6
  28.3 186.7 %all-to-all-start.6 = ((bf16[2,32,128,896]{3,2,0,1:T(8,128)(2,1)}), bf16[2,32,128,896]{3,2,0,1:T(8,128)(2,1)}, u32[]{:S(2)}, u32[]{:S(2)}) async-start(bf16[2,32,128,896]{3,2,0,1:T(8,128)(2,1)} %copy.130), calls=%async_computation.6 | async-start | bytes 29360128 | tf_op jit(solution)/shard_map/all_to_all | solution.py:51
  215.0 205.8 %all-to-all-start.2 = ((bf16[2,32,128,896]{3,2,0,1:T(8,128)(2,1)}), bf16[2,32,128,896]{3,2,0,1:T(8,128)(2,1)}, u32[]{:S(2)}, u32[]{:S(2)}) async-start(bf16[2,32,128,896]{3,2,0,1:T(8,128)(2,1)} %copy.112), calls=%async_computation.2 | async-start | bytes 29360128 | tf_op jit(solution)/shard_map/all_to_all | solution.py:51
  252.4 196.0 %copy-start.5 = (bf16[2,256,896]{2,1,0:T(8,128)(2,1)S(1)}, bf16[2,256,896]{2,1,0:T(8,128)(2,1)}, u32[]{:S(2)}) copy-start(bf16[2,256,896]{2,1,0:T(8,128)(2,1)} %param.15) | copy-start | bytes 2752516
  420.8 195.0 %all-to-all-start = ((bf16[2,32,128,896]{3,2,0,1:T(8,128)(2,1)}), bf16[2,32,128,896]{3,2,0,1:T(8,128)(2,1)}, u32[]{:S(2)}, u32[]{:S(2)}) async-start(bf16[2,32,128,896]{3,2,0,1:T(8,128)(2,1)} %copy.103), calls=%async_computation | async-start | bytes 29360128 | tf_op jit(solution)/shard_map/all_to_all | solution.py:51
  460.7 181.2 %copy-start.13 = (s32[2,256,8]{1,2,0:T(8,128)S(1)}, s32[2,256,8]{1,2,0:T(8,128)}, u32[]{:S(2)}) copy-start(s32[2,256,8]{1,2,0:T(8,128)} %param.10) | copy-start | bytes 49156
  615.9 206.4 %all-to-all-start.4 = ((bf16[2,32,128,896]{3,2,0,1:T(8,128)(2,1)}), bf16[2,32,128,896]{3,2,0,1:T(8,128)(2,1)}, u32[]{:S(2)}, u32[]{:S(2)}) async-start(bf16[2,32,128,896]{3,2,0,1:T(8,128)(2,1)} %copy.121), calls=%async_computation.4 | async-start | bytes 29360128 | tf_op jit(solution)/shard_map/all_to_all | solution.py:51
  647.7 13.7 copy-start.17
  661.4 18.6 %copy-start.14 = (bf16[2,896,640]{2,1,0:T(8,128)(2,1)S(1)}, bf16[2,896,640]{2,1,0:T(8,128)(2,1)}, u32[]{:S(2)}) copy-start(bf16[2,896,640]{2,1,0:T(8,128)(2,1)} %param.12) | copy-start | bytes 6881284
  822.2 198.3 %all-to-all-start.3 = ((bf16[2,32,128,896]{3,2,0,1:T(8,128)(2,1)}), bf16[2,32,128,896]{3,2,0,1:T(8,128)(2,1)}, u32[]{:S(2)}, u32[]{:S(2)}) async-start(bf16[2,32,128,896]{3,2,0,1:T(8,128)(2,1)} %copy.114), calls=%async_computation.3 | async-start | bytes 29360128 | tf_op jit(solution)/shard_map/all_to_all | solution.py:51
  861.1 13.8 copy-start.15
  1020.5 199.2 %all-to-all-start.1 = ((bf16[2,32,128,896]{3,2,0,1:T(8,128)(2,1)}), bf16[2,32,128,896]{3,2,0,1:T(8,128)(2,1)}, u32[]{:S(2)}, u32[]{:S(2)}) async-start(bf16[2,32,128,896]{3,2,0,1:T(8,128)(2,1)} %copy.105), calls=%async_computation.1 | async-start | bytes 29360128 | tf_op jit(solution)/shard_map/all_to_all | solution.py:51
  1070.1 22.0 %copy-start.18 = (bf16[2,896,640]{2,1,0:T(8,128)(2,1)S(1)}, bf16[2,896,640]{2,1,0:T(8,128)(2,1)}, u32[]{:S(2)}) copy-start(bf16[2,896,640]{2,1,0:T(8,128)(2,1)} %param.13) | copy-start | bytes 6881284
  1130.3 114.3 %copy-start.16 = (bf16[2,896,640]{2,1,0:T(8,128)(2,1)S(1)}, bf16[2,896,640]{2,1,0:T(8,128)(2,1)}, u32[]{:S(2)}) copy-start(bf16[2,896,640]{2,1,0:T(8,128)(2,1)} %param.12) | copy-start | bytes 6881284
  1219.7 205.3 %all-to-all-start.7 = ((bf16[2,32,128,896]{3,2,0,1:T(8,128)(2,1)}), bf16[2,32,128,896]{3,2,0,1:T(8,128)(2,1)}, u32[]{:S(2)}, u32[]{:S(2)}) async-start(bf16[2,32,128,896]{3,2,0,1:T(8,128)(2,1)} %copy.132), calls=%async_computation.7 | async-start | bytes 29360128 | tf_op jit(solution)/shard_map/all_to_all | solution.py:51
  1425.0 199.1 %all-to-all-start.5 = ((bf16[2,32,128,896]{3,2,0,1:T(8,128)(2,1)}), bf16[2,32,128,896]{3,2,0,1:T(8,128)(2,1)}, u32[]{:S(2)}, u32[]{:S(2)}) async-start(bf16[2,32,128,896]{3,2,0,1:T(8,128)(2,1)} %copy.123), calls=%async_computation.5 | async-start | bytes 29360128 | tf_op jit(solution)/shard_map/all_to_all | solution.py:51
  1501.2 13.6 copy-start.4
  1514.7 17.5 %copy-start.10 = (bf16[256,896,1]{1,0,2:T(8,128)(2,1)S(1)}, bf16[256,896,1]{1,0,2:T(8,128)(2,1)}, u32[]{:S(2)}) copy-start(bf16[256,896,1]{1,0,2:T(8,128)(2,1)} %get-tuple-element.19) | copy-start | bytes 1376260
  1514.7 17.5 %copy-start.12 = (pred[256,8]{1,0:T(8,128)(4,1)S(1)}, pred[256,8]{1,0:T(8,128)(4,1)}, u32[]{:S(2)}) copy-start(pred[256,8]{1,0:T(8,128)(4,1)} %copy.111) | copy-start | bytes 6148
  1537.4 14.0 copy-start.3
  1551.3 17.6 %copy-start.9 = (bf16[256,896,1]{1,0,2:T(8,128)(2,1)S(1)}, bf16[256,896,1]{1,0,2:T(8,128)(2,1)}, u32[]{:S(2)}) copy-start(bf16[256,896,1]{1,0,2:T(8,128)(2,1)} %get-tuple-element.18) | copy-start | bytes 1376260
  1551.4 17.6 %copy-start.11 = (pred[256,8]{1,0:T(8,128)(4,1)S(1)}, pred[256,8]{1,0:T(8,128)(4,1)}, u32[]{:S(2)}) copy-start(pred[256,8]{1,0:T(8,128)(4,1)} %copy.102) | copy-start | bytes 6148
  1587.6 22.5 %copy-start.8 = (f32[256,8]{1,0:T(8,128)S(1)}, f32[256,8]{1,0:T(8,128)}, u32[]{:S(2)}) copy-start(f32[256,8]{1,0:T(8,128)} %copy.108) | copy-start | bytes 24580
  1587.6 27.5 %copy-start.7 = (f32[256,8]{1,0:T(8,128)S(1)}, f32[256,8]{1,0:T(8,128)}, u32[]{:S(2)}) copy-start(f32[256,8]{1,0:T(8,128)} %copy.99) | copy-start | bytes 24580
  1605.1 9.9 copy-start.2
  1637.7 25.4 %copy-start.1 = (bf16[2,640,896]{2,1,0:T(8,128)(2,1)S(1)}, bf16[2,640,896]{2,1,0:T(8,128)(2,1)}, u32[]{:S(2)}) copy-start(bf16[2,640,896]{2,1,0:T(8,128)(2,1)} %param.14) | copy-start | bytes 6881284
where the time goes:
time: 1690 us; the launch traced here: 1660 us
  waiting for transfers between devices  767 us (45%)
  matrix products  416 us (25%)
  local copies, waits for them, and re-layouts  288 us (17%)
  starting transfers between devices  165 us (10%)
  other arithmetic  25.8 us (2%)
    all_to_all x8, waiting for transfers between devices, exchange(): return lax.all_to_all(send_buf, GROUP_AXES, 1, 1, tiled=True)  767 us
    all_to_all x8, starting transfers between devices, exchange(): return lax.all_to_all(send_buf, GROUP_AXES, 1, 1, tiled=True)  165 us
    all_to_all x8, local copies, waits for them, and re-layouts, exchange(): return lax.all_to_all(send_buf, GROUP_AXES, 1, 1, tiled=True)  109 us
    dot_general x2, matrix products, expert_backward(): jnp.einsum('lnd,lfd->lnf', d_out, w_down, preferred_element_type=jnp.floa...  63.8 us
    dot_general x2, matrix products, expert_backward(): jnp.einsum('lnf,ldf->lnd', d_up, w_up, preferred_element_type=jnp.float32)  50.1 us
    dot_general x2, matrix products, expert_backward(): jnp.einsum('lnf,ldf->lnd', d_gate, w_gate, preferred_element_type=jnp.flo...  42.2 us
    dot_general x2, matrix products, expert_forward(): jnp.einsum('lnf,lfd->lnd', hidden, w_down, preferred_element_type=jnp.flo...  41.3 us
    dot_general x2, matrix products, expert_backward(): jnp.einsum('lnd,lnf->ldf', x_rows, d_up, preferred_element_type=jnp.float32)  38.2 us
  transfers between devices with their start and end apart: 8, of which 8 were waited for; matrix products, arithmetic and copies ran while one was open for 40% of the time, Pallas kernels for 0%

commit v1 on v0

v1 whole, which is shorter than its diff:
```python
import functools

import jax
import jax.numpy as jnp
from jax import lax
from jax.experimental import pallas as pl
from jax.experimental.pallas import tpu as pltpu
from jax.sharding import PartitionSpec as P

GROUP_AXES = ("row", "col", "core")
ALL_AXES = ("rep", "row", "col", "core")
TILE = 256
LANES = 128


def expert_kernel(dims, first, *refs):
    nblk, span, tok, model, ff, experts, cap = dims
    nsup = nblk // span
    seg, last_row, tiles, pos_rows, tokens, cols_hbm, wgu_hbm, wd_hbm, wdt_hbm, wgut_hbm = refs[:10]
    refs = refs[10:]
    if not first:
        prev, refs = refs[:3], refs[3:]
    out_hbm, dg_hbm, gg_hbm, gu_hbm, gd_hbm = refs[:5]
    (rows_x, rows_q, wgu, wd, wdt, wgut, acc_gu, acc_d, xbuf, dybuf, colbuf, outbuf, dgbuf, dh, sem_x, sem_dy, sem_c,
     sem_w, sem_a, sem_out, sem_dg) = refs[5:]

    def x_copy(s):
        return pltpu.make_async_copy(tokens.at[0, pl.ds(s * span * tok, span * tok)], xbuf, sem_x)

    def dy_copy(s, slot):
        return pltpu.make_async_copy(tokens.at[1, pl.ds(s * span * tok, span * tok)], dybuf.at[slot], sem_dy.at[slot])

    def col_copy(s, slot):
        return pltpu.make_async_copy(cols_hbm.at[pl.ds(s * span * tok, span * tok)], colbuf.at[slot], sem_c.at[slot])

    def out_copies(blk, slot):
        where = pl.ds(blk * tok, tok)
        return (pltpu.make_async_copy(outbuf.at[slot], out_hbm.at[where], sem_out.at[slot]),
                pltpu.make_async_copy(dgbuf.at[slot], dg_hbm.at[where], sem_dg.at[slot]))

    weights = [pltpu.make_async_copy(src, dst, sem_w.at[i])
               for i, (src, dst) in enumerate(((wgu_hbm, wgu), (wd_hbm, wd), (wdt_hbm, wdt), (wgut_hbm, wgut)))]
    sums = (acc_gu.at[:, :, pl.ds(0, ff)], acc_gu.at[:, :, pl.ds(ff, ff)], acc_d)

    x_copy(0).start()
    dy_copy(0, 0).start()
    col_copy(0, 0).start()
    for copy in weights:
        copy.start()
    if first:
        for e in range(experts):
            @pl.loop(0, model // 128)
            def _(i, e=e):
                acc_gu[e, pl.ds(i * 128, 128), :] = jnp.zeros((128, 2 * ff), jnp.float32)

            @pl.loop(0, ff // 128)
            def _(i, e=e):
                acc_d[e, pl.ds(i * 128, 128), :] = jnp.zeros((128, model), jnp.float32)
    else:
        for i, (src, dst) in enumerate(zip(prev, sums)):
            pltpu.make_async_copy(src, dst, sem_a.at[i]).start()

    def step(s, carry):
        slot = lax.rem(s, 2)
        x_copy(s).wait()
        dy_copy(s, slot).wait()
        col_copy(s, slot).wait()

        @pl.when(s + 1 < nsup)
        def _():
            dy_copy(s + 1, 1 - slot).start()
            col_copy(s + 1, 1 - slot).start()

        def pack(b, carry):
            rows = pl.ds(pl.multiple_of(b * tok, tok), tok)
            blk = s * span + b
            x_b = xbuf[rows, :]
            dy_b = dybuf[slot, rows, :].astype(jnp.float32)
            for e in range(experts):
                gate = colbuf[slot, rows, e:e + 1]
                q_b = (gate * dy_b).astype(jnp.bfloat16)
                hit = lax.broadcasted_iota(jnp.int32, (cap, tok), 0) == pos_rows[e, pl.ds(blk, 1), :]
                pick = jnp.where(hit, 1.0, 0.0).astype(jnp.bfloat16)
                at = pl.ds(pl.multiple_of(seg[e, blk], 16), cap)
                rows_x[e, at, :] = jnp.dot(pick, x_b, preferred_element_type=jnp.float32).astype(jnp.bfloat16)
                rows_q[e, at, :] = jnp.dot(pick, q_b, preferred_element_type=jnp.float32).astype(jnp.bfloat16)
            return carry

        lax.fori_loop(0, span, pack, 0)
        for e in range(experts):
            tail = pl.ds(pl.multiple_of(last_row[e, s], 16), TILE)
            rows_x[e, tail, :] = jnp.zeros((TILE, model), jnp.bfloat16)
            rows_q[e, tail, :] = jnp.zeros((TILE, model), jnp.bfloat16)

        @pl.when(s + 1 < nsup)
        def _():
            x_copy(s + 1).start()

        @pl.when(s == 0)
        def _():
            for copy in weights:
                copy.wait()
            if not first:
                for i, (src, dst) in enumerate(zip(prev, sums)):
                    pltpu.make_async_copy(src, dst, sem_a.at[i]).wait()

        def expert(e, carry):
            def tile(i, carry):
                at = pl.ds(pl.multiple_of(i * TILE, TILE), TILE)
                x_t = rows_x[e, at, :]
                q_t = rows_q[e, at, :]
                u = jnp.dot(x_t, wgu[e, :, 0:ff], preferred_element_type=jnp.float32).astype(jnp.bfloat16).astype(jnp.float32)
                v = jnp.dot(x_t, wgu[e, :, ff:2 * ff], preferred_element_type=jnp.float32).astype(jnp.bfloat16).astype(jnp.float32)
                r = jnp.dot(q_t, wdt[e], preferred_element_type=jnp.float32)
                sig = jax.nn.sigmoid(u)
                us = u * sig
                hidden = (us * v).astype(jnp.bfloat16)
                dh[:, 0:ff] = (r * v * sig * (1.0 + u * (1.0 - sig))).astype(jnp.bfloat16)
                dh[:, ff:2 * ff] = (r * us).astype(jnp.bfloat16)
                d_t = dh[...]
                over_rows = (((0,), (0,)), ((), ()))
                acc_gu[e] += lax.dot_general(x_t, d_t, over_rows, preferred_element_type=jnp.float32)
                acc_d[e] += lax.dot_general(hidden, q_t, over_rows, preferred_element_type=jnp.float32)
                rows_x[e, at, :] = jnp.dot(hidden, wd[e], preferred_element_type=jnp.float32).astype(jnp.bfloat16)
                rows_q[e, at, :] = jnp.dot(d_t, wgut[e], preferred_element_type=jnp.float32).astype(jnp.bfloat16)
                return carry

            lax.fori_loop(0, tiles[e, s], tile, 0)
            return carry

        lax.fori_loop(0, experts, expert, 0)

        def unpack(b, carry):
            rows = pl.ds(pl.multiple_of(b * tok, tok), tok)
            blk = s * span + b
            o_slot = lax.rem(blk, 2)

            @pl.when(blk >= 2)
            def _():
                for copy in out_copies(blk - 2, o_slot):
                    copy.wait()

            dy_b = dybuf[slot, rows, :].astype(jnp.float32)
            y_b = gx_b = None
            for e in range(experts):
                at = pl.ds(pl.multiple_of(seg[e, blk], 16), cap)
                hit = lax.broadcasted_iota(jnp.int32, (tok, cap), 1).astype(jnp.float32) == colbuf[slot, rows, experts + e:experts + e + 1]
                put = jnp.where(hit, 1.0, 0.0).astype(jnp.bfloat16)
                o_b = jnp.dot(put, rows_x[e, at, :], preferred_element_type=jnp.float32)
                p_b = jnp.dot(put, rows_q[e, at, :], preferred_element_type=jnp.float32)
                dgbuf[o_slot, :, e:e + 1] = jnp.sum(dy_b * o_b, axis=1, keepdims=True)
                o_b = colbuf[slot, rows, e:e + 1] * o_b
                y_b = o_b if y_b is None else y_b + o_b
                gx_b = p_b if gx_b is None else gx_b + p_b
            outbuf[o_slot, :, 0:model] = y_b
            outbuf[o_slot, :, model:2 * model] = gx_b
            for copy in out_copies(blk, o_slot):
                copy.start()
            return carry

        lax.fori_loop(0, span, unpack, 0)
        return carry

    lax.fori_loop(0, nsup, step, 0)
    outs = [pltpu.make_async_copy(src, dst, sem_a.at[i]) for i, (src, dst) in enumerate(zip(sums, (gg_hbm, gu_hbm, gd_hbm)))]
    for copy in outs:
        copy.start()
    for blk in (nblk - 2, nblk - 1):
        for copy in out_copies(blk, blk % 2):
            copy.wait()
    for copy in outs:
        copy.wait()


def tables(gate):
    micro, nblk, experts, tok = gate.shape
    span = blocks_per_step(nblk)
    gate = jnp.transpose(gate, (0, 2, 1, 3))
    chosen = gate >= 0.0
    before = jnp.triu(jnp.ones((tok, tok), jnp.bfloat16), 1)
    pos = jnp.einsum("mlgt,tu->mlgu", chosen.astype(jnp.bfloat16), before, preferred_element_type=jnp.float32)
    pos = jnp.where(chosen, pos, -1.0)
    count = jnp.sum(chosen.astype(jnp.int32), axis=3)
    room = ((count + 15) // 16 * 16).reshape(micro, experts, nblk // span, span)
    ends = jnp.cumsum(room, axis=3)
    seg = (ends - room).reshape(micro, experts, nblk)
    last_row = ends[..., -1]
    cols = jnp.concatenate([jnp.maximum(gate, 0.0), pos], axis=1).reshape(micro, 2 * experts, nblk * tok)
    cols = jnp.pad(jnp.transpose(cols, (0, 2, 1)), ((0, 0), (0, 0), (0, LANES - 2 * experts)))
    made = (seg, last_row, (last_row + TILE - 1) // TILE, pos.astype(jnp.int32), cols)
    return lax.optimization_barrier([tuple(table[m] for table in made) for m in range(micro)])


def blocks_per_step(nblk):
    return 8 if nblk % 8 == 0 else nblk


def run_experts(made, tokens, weights, prev):
    seg, last_row, tiles, pos, cols = made
    experts, nblk, tok = pos.shape
    model, ff = weights[0].shape[1], weights[1].shape[1]
    cap = tok // 2
    span = blocks_per_step(nblk)
    rows = nblk * tok
    f32, bf16 = jnp.float32, jnp.bfloat16
    packed = span * cap + TILE
    smem, anywhere = pl.BlockSpec(memory_space=pltpu.SMEM), pl.BlockSpec(memory_space=pl.ANY)
    vmem = pl.BlockSpec(memory_space=pltpu.VMEM)
    first = prev is None
    args = [seg, last_row, tiles, pos, tokens, cols, *weights] + ([] if first else list(prev))
    dims = (nblk, span, tok, model, ff, experts, cap)
    return pl.pallas_call(
        functools.partial(expert_kernel, dims, first),
        name="experts_first" if first else "experts_next",
        out_shape=(jax.ShapeDtypeStruct((rows, 2 * model), f32),
                   jax.ShapeDtypeStruct((rows, LANES), f32), jax.ShapeDtypeStruct((experts, model, ff), f32),
                   jax.ShapeDtypeStruct((experts, model, ff), f32), jax.ShapeDtypeStruct((experts, ff, model), f32)),
        in_specs=[smem] * 3 + [vmem] + [anywhere] * (len(args) - 4),
        out_specs=(anywhere,) * 5,
        scratch_shapes=[
            pltpu.VMEM((experts, packed, model), bf16), pltpu.VMEM((experts, packed, model), bf16),
            pltpu.VMEM((experts, model, 2 * ff), bf16), pltpu.VMEM((experts, ff, model), bf16),
            pltpu.VMEM((experts, model, ff), bf16), pltpu.VMEM((experts, 2 * ff, model), bf16),
            pltpu.VMEM((experts, model, 2 * ff), f32), pltpu.VMEM((experts, ff, model), f32),
            pltpu.VMEM((span * tok, model), bf16), pltpu.VMEM((2, span * tok, model), bf16),
            pltpu.VMEM((2, span * tok, LANES), f32),
            pltpu.VMEM((2, tok, 2 * model), f32), pltpu.VMEM((2, tok, LANES), f32),
            pltpu.VMEM((TILE, 2 * ff), bf16),
            pltpu.SemaphoreType.DMA, pltpu.SemaphoreType.DMA((2,)), pltpu.SemaphoreType.DMA((2,)),
            pltpu.SemaphoreType.DMA((4,)), pltpu.SemaphoreType.DMA((3,)),
            pltpu.SemaphoreType.DMA((2,)), pltpu.SemaphoreType.DMA((2,)),
        ],
        compiler_params=pltpu.CompilerParams(vmem_limit_bytes=66 * 1000 * 1000),
        cost_estimate=pl.CostEstimate(flops=18 * rows * model * ff, bytes_accessed=12 * rows * model, transcendentals=rows * ff),
    )(*args)


def solution(mesh):
    group_size = mesh.shape["row"] * mesh.shape["col"] * mesh.shape["core"]
    tok_spec = P(None, ALL_AXES, None)
    w_spec = P(ALL_AXES, None, None)

    def moe_layer(x, route_idx, gates, w_gate, w_up, w_down, grad_y):
        micro, tok = x.shape[0], x.shape[1]
        local = w_gate.shape[0]
        gathered = [lax.all_gather(jnp.stack([x[m], grad_y[m]]), GROUP_AXES, axis=1, tiled=True) for m in range(micro)]
        route_t = jnp.transpose(route_idx, (0, 2, 1))
        gates_t = jnp.transpose(gates, (0, 2, 1))
        hits = route_t[:, :, None, :] == jnp.arange(group_size * local)[None, None, :, None]
        table = jnp.where(jnp.any(hits, axis=1), jnp.sum(jnp.where(hits, gates_t[:, :, None, :], 0.0), axis=1), -1.0)
        made = tables(lax.all_to_all(table.reshape(micro, group_size, local, tok), GROUP_AXES, 1, 1, tiled=True))
        weights = (jnp.concatenate([w_gate, w_up], axis=2), w_down, jnp.transpose(w_down, (0, 2, 1)),
                   jnp.concatenate([jnp.transpose(w_gate, (0, 2, 1)), jnp.transpose(w_up, (0, 2, 1))], axis=1))
        outs_y, outs_dx, outs_dg = [], [], []
        sums = None
        for m in range(micro):
            part, part_dg, *sums = run_experts(made[m], gathered[m], weights, sums)
            whole = lax.psum_scatter(part, GROUP_AXES, scatter_dimension=0, tiled=True).astype(x.dtype)
            outs_y.append(whole[:, :x.shape[2]])
            outs_dx.append(whole[:, x.shape[2]:])
            part_dg = jnp.transpose(part_dg[:, :local].reshape(group_size, tok, local), (0, 2, 1))
            by_expert = lax.all_to_all(part_dg, GROUP_AXES, 0, 0, tiled=True).reshape(group_size * local, tok)
            outs_dg.append(jnp.sum(jnp.where(hits[m], by_expert[None], 0.0), axis=1).T)
        return (jnp.stack(outs_y), jnp.stack(outs_dx), jnp.stack(outs_dg), *sums)

    return jax.shard_map(moe_layer, mesh=mesh, in_specs=(tok_spec, tok_spec, tok_spec, w_spec, w_spec, w_spec, tok_spec), out_specs=(tok_spec, tok_spec, tok_spec, w_spec, w_spec, w_spec), check_vma=False)
```

time: 1690 us -> 769 us (0.46); the launches traced: 1660 us -> 768 us
  matrix products: 416 us -> 0.17 us
  waiting for transfers between devices: 767 us -> 396 us
  local copies, waits for them, and re-layouts: 288 us -> 41.9 us
  Pallas kernels: 0 us -> 218 us
  starting transfers between devices: 165 us -> 85.2 us
    all_to_all x8 -> x3, waiting for transfers between devices: 767 us -> 11.7 us  [the longest x2 11.7 us: moe_layer(): lax.all_to_all(part_dg, GROUP_AXES, 0, 0, tiled=True)]
    dot_general x24 -> x1, matrix products: 416 us -> 0.17 us  [tables(): jnp.einsum('mlgt,tu->mlgu', chosen.astype(jnp.bfloat16), before, preferre...]
    reduce_scatter x0 -> x2, waiting for transfers between devices: none -> 330 us  [moe_layer(): lax.psum_scatter(part, GROUP_AXES, scatter_dimension=0, tiled=True)]
    pallas_call x0 -> x2, Pallas kernels: none -> 218 us  [run_experts(): pl.pallas_call(functools.partial(expert_kernel, dims, first), name='exper...]
    all_to_all x8 -> x0, local copies, waits for them, and re-layouts: 109 us -> none  [exchange(): return lax.all_to_all(send_buf, GROUP_AXES, 1, 1, tiled=True)]
    all_to_all x8 -> x3, starting transfers between devices: 165 us -> 84.7 us  [the longest x2 75.6 us: moe_layer(): lax.all_to_all(part_dg, GROUP_AXES, 0, 0, tiled=True)]
    gather x4 -> x0, local copies, waits for them, and re-layouts: 70.3 us -> none  [the longest x2 35.2 us: moe_layer(): jnp.take(dx_back, slot_addr, axis=0).astype(jnp.float32)]
    all_gather x0 -> x2, waiting for transfers between devices: none -> 54.3 us  [moe_layer(): lax.all_gather(jnp.stack([x[m], grad_y[m]]), GROUP_AXES, axis=1, tiled=True)]
  transfers between devices with their start and end apart: 8 -> 7, of which waited for: 8 -> 5; matrix products, arithmetic and copies ran while one was open for 40% -> 6% of each run, Pallas kernels for 0% -> 28%
where the time goes in v1:
time: 769 us; the launch traced here: 768 us
  waiting for transfers between devices  396 us (51%)
  Pallas kernels  218 us (28%)
  starting transfers between devices  85.2 us (11%)
  local copies, waits for them, and re-layouts  41.9 us (5%)
  between operations  14 us (2%)
  other arithmetic  12.7 us (2%)
    reduce_scatter x2, waiting for transfers between devices, moe_layer(): lax.psum_scatter(part, GROUP_AXES, scatter_dimension=0, tiled=True)  330 us
    pallas_call x2, Pallas kernels, run_experts(): pl.pallas_call(functools.partial(expert_kernel, dims, first), name='exper...  218 us
    all_to_all x2, starting transfers between devices, moe_layer(): lax.all_to_all(part_dg, GROUP_AXES, 0, 0, tiled=True)  75.6 us
    all_gather x2, waiting for transfers between devices, moe_layer(): lax.all_gather(jnp.stack([x[m], grad_y[m]]), GROUP_AXES, axis=1, tiled=True)  54.3 us
  transfers between devices with their start and end apart: 7, of which 5 were waited for; matrix products, arithmetic and copies ran while one was open for 6% of the time, Pallas kernels for 28%

profile of v1, /device:TPU:97, one launch (start us, length us, event | category | flops | bytes accessed | tf_op | source)
XLA Modules:
  0.0 768.3 jit_solution(6173765794402344729)
XLA Ops:
  7.2 0.0 copy-start.4
  7.2 0.0 copy-start.3
  7.2 0.1 all-gather.3.cloned.1.call-start
  7.3 1.6 fusion.15
  8.9 1.0 pad_maximum_fusion.1
  9.9 0.1 all-gather.3.cloned.1.call-update
  9.9 0.1 all-gather.5.cloned.1.call-start
  10.0 1.0 pad_maximum_fusion.2
  11.0 0.1 all-gather.5.cloned.1.call-update
  11.1 0.0 copy-done.4
  11.1 0.0 copy-done.3
  11.1 0.1 select_reduce_fusion
  11.2 0.9 iota_compare_fusion
  12.2 0.1 copy.33
  12.3 0.7 copy.34
  13.0 9.1 %all-to-all-start = ((f32[2,32,2,256]{3,2,0,1:T(2,128)}), f32[2,32,2,256]{3,2,0,1:T(2,128)S(1)}, u32[]{:S(2)}, u32[]{:S(2)}) async-start(f32[2,32,2,256]{3,2,0,1:T(2,128)} %copy.34), calls=%async_computation | async-start | bytes 262144 | tf_op jit(solution)/shard_map/all_to_all | solution.py:251
  22.1 0.1 reduce-scatter.3.cloned.1.call-start
  22.2 3.2 copy.39
  25.4 4.3 copy.40
  29.7 4.3 copy.38
  34.0 0.0 copy-start
  34.0 3.5 constant_dynamic-update-slice_fusion.1
  37.4 0.0 copy-done
  37.4 2.4 pad_maximum_fusion.refs_9_
  39.9 0.0 copy-done.1
  39.9 1.6 constant_dynamic-update-slice_fusion.refs_6_
  41.5 0.0 all-to-all-done
  41.5 0.2 convert_reduce_fusion
  41.6 0.1 add.28
  41.8 0.7 reduce_window_sum.11
  42.5 0.6 squeeze.42.refs_0_
  43.2 0.6 squeeze.37.refs_0_
  43.8 0.2 fusion.18
  44.0 4.7 copy.37
  48.7 0.8 slice_reduce_fusion
  49.5 0.2 fusion.11
  49.7 0.6 slice_bitcast_fusion.8
  50.3 0.7 slice_bitcast_fusion.6
  50.9 7.4 fusion.1
  58.3 54.3 %all-gather.3.cloned.1.call-done.refs_4_ = bf16[2,8192,896]{2,1,0:T(8,128)(2,1)} async-done(((bf16[2,256,896]{2,1,0:T(8,128)(2,1)}), bf16[2,8192,896]{2,1,0:T(8,128)(2,1)}) %all-gather.3.cloned.1.call-update) | async-done | bytes 29360144 | tf_op jit(solution)/shard_map/all_gather | solution.py:246
  112.7 107.8 %experts_first.1 = (f32[8192,1792]{1,0:T(8,128)}, f32[8192,128]{1,0:T(8,128)}, f32[2,896,640]{2,1,0:T(8,128)}, f32[2,896,640]{2,1,0:T(8,128)}, f32[2,640,896]{2,1,0:T(8,128)}) custom-call(s32[2,32]{1,0:T(2,128)} %squeeze.37.refs_0_, s32[2,4]{1,0:T(2,128)} %get-tuple-element.27.refs_1_, s32[2,4]{1,0:T(2,128)} %get-tuple-element.28.refs_2_, ...), custom_call_target="tpu_custom_call" | custom-call | flops 84557168640 | bytes 88080384 | tf_op jit(solution)/shard_map/experts_first/pallas_call | solution.py:212
  220.5 0.1 reduce-scatter.3.cloned.1.call-update
  220.5 0.2 reduce-scatter.5.cloned.1.call-start
  220.8 0.0 all-gather.5.cloned.1.call-done.refs_4_
  220.8 110.7 %experts_next.1 = (f32[8192,1792]{1,0:T(8,128)}, f32[8192,128]{1,0:T(8,128)}, f32[2,896,640]{2,1,0:T(8,128)}, f32[2,896,640]{2,1,0:T(8,128)}, f32[2,640,896]{2,1,0:T(8,128)}) custom-call(s32[2,32]{1,0:T(2,128)} %squeeze.42.refs_0_, s32[2,4]{1,0:T(2,128)} %get-tuple-element.33.refs_1_, s32[2,4]{1,0:T(2,128)} %get-tuple-element.34.refs_2_, ...), custom_call_target="tpu_custom_call" | custom-call | flops 84557168640 | bytes 88080384 | tf_op jit(solution)/shard_map/experts_next/pallas_call | solution.py:212
  331.5 0.1 reduce-scatter.5.cloned.1.call-update
  331.5 0.0 copy-start.2
  331.5 3.5 copy.41
  335.0 72.7 %all-to-all-start.1 = ((f32[32,2,256]{2,1,0:T(2,128)}), f32[32,2,256]{2,1,0:T(2,128)S(1)}, u32[]{:S(2)}, u32[]{:S(2)}) async-start(f32[32,2,256]{2,1,0:T(2,128)} %bitcast.24), calls=%async_computation.3 | async-start | bytes 131072 | tf_op jit(solution)/shard_map/all_to_all | solution.py:262
  407.8 3.5 copy.42
  411.2 4.1 all-to-all-done.1
  415.3 2.9 all-to-all-start.2
  418.2 7.7 all-to-all-done.2
  426.0 0.0 copy-done.2
  426.0 0.2 select_reduce_fusion.2
  426.1 0.6 pad_maximum_fusion.6
  426.8 92.2 %reduce-scatter.3.cloned.1.call-done = f32[256,1792]{1,0:T(8,128)} async-done(((f32[8192,1792]{1,0:T(8,128)}), f32[256,1792]{1,0:T(8,128)}) %reduce-scatter.3.cloned.1.call-update) | async-done | bytes 1835024 | tf_op jit(solution)/shard_map/reduce_scatter | solution.py:258
  518.9 1.6 convert_element_type.17
  520.5 0.1 slice_bitcast_fusion.3
  520.6 237.5 %reduce-scatter.5.cloned.1.call-done = f32[256,1792]{1,0:T(8,128)} async-done(((f32[8192,1792]{1,0:T(8,128)}), f32[256,1792]{1,0:T(8,128)}) %reduce-scatter.5.cloned.1.call-update) | async-done | bytes 1835024 | tf_op jit(solution)/shard_map/reduce_scatter | solution.py:258
  758.1 1.6 convert_element_type.18
  759.7 0.1 slice_bitcast_fusion.2
  759.7 1.0 pad_maximum_fusion.4
  760.8 1.0 pad_maximum_fusion.3
  (11 shorter events, 0.2 us)
Async XLA Ops:
  7.2 3.9 copy-start.4
  7.2 3.9 copy-start.3
  7.2 105.5 %all-gather.3.cloned.1.call-start = ((), (), s32[]{:S(2)}) async-start(), calls=%async_computation.5 | async-start | bytes 30277632 | tf_op jit(solution)/shard_map/all_gather | solution.py:246
  9.9 210.9 %all-gather.5.cloned.1.call-start = ((), (), s32[]{:S(2)}) async-start(), calls=%async_computation.7 | async-start | bytes 30277632 | tf_op jit(solution)/shard_map/all_gather | solution.py:246
  13.0 28.5 %all-to-all-start = ((f32[2,32,2,256]{3,2,0,1:T(2,128)}), f32[2,32,2,256]{3,2,0,1:T(2,128)S(1)}, u32[]{:S(2)}, u32[]{:S(2)}) async-start(f32[2,32,2,256]{3,2,0,1:T(2,128)} %copy.34), calls=%async_computation | async-start | bytes 262144 | tf_op jit(solution)/shard_map/all_to_all | solution.py:251
  22.1 496.8 %reduce-scatter.3.cloned.1.call-start = ((), (), s32[]{:S(2)}) async-start(), calls=%async_computation.6 | async-start | bytes 60555264 | tf_op jit(solution)/shard_map/reduce_scatter | solution.py:258
  34.0 3.5 copy-start
  37.4 2.4 copy-start.1
  220.5 537.5 %reduce-scatter.5.cloned.1.call-start = ((), (), s32[]{:S(2)}) async-start(), calls=%async_computation.8 | async-start | bytes 60555264 | tf_op jit(solution)/shard_map/reduce_scatter | solution.py:258
  331.5 94.4 %copy-start.2 = (pred[2,8,64,256]{3,2,1,0:T(8,128)(4,1)S(1)}, pred[2,8,64,256]{3,2,1,0:T(8,128)(4,1)}, u32[]{:S(2)}) copy-start(pred[2,8,64,256]{3,2,1,0:T(8,128)(4,1)} %get-tuple-element.64) | copy-start | bytes 786436
  335.0 80.3 %all-to-all-start.1 = ((f32[32,2,256]{2,1,0:T(2,128)}), f32[32,2,256]{2,1,0:T(2,128)S(1)}, u32[]{:S(2)}, u32[]{:S(2)}) async-start(f32[32,2,256]{2,1,0:T(2,128)} %bitcast.24), calls=%async_computation.3 | async-start | bytes 131072 | tf_op jit(solution)/shard_map/all_to_all | solution.py:262
  415.3 10.6 %all-to-all-start.2 = ((f32[32,2,256]{2,1,0:T(2,128)}), f32[32,2,256]{2,1,0:T(2,128)S(1)}, u32[]{:S(2)}, u32[]{:S(2)}) async-start(f32[32,2,256]{2,1,0:T(2,128)} %bitcast.29), calls=%async_computation.4 | async-start | bytes 131072 | tf_op jit(solution)/shard_map/all_to_all | solution.py:262
Sparse Core Ops, SparseCore 0:
  10.7 101.8 all-gather.2
  115.3 96.6 all-gather.4
  220.7 298.2 reduce-scatter.2
  522.6 235.4 reduce-scatter.4

commit v2 on v1

--- a/solution.py
+++ b/solution.py
@@ -11,6 +11,7 @@
 ALL_AXES = ("rep", "row", "col", "core")
 TILE = 256
 LANES = 128
+HALVES = 2
 
 
 def expert_kernel(dims, first, *refs):
@@ -174,7 +175,7 @@
 
 def tables(gate):
     micro, nblk, experts, tok = gate.shape
-    span = blocks_per_step(nblk)
+    span = blocks_per_step(nblk, tok)
     gate = jnp.transpose(gate, (0, 2, 1, 3))
     chosen = gate >= 0.0
     before = jnp.triu(jnp.ones((tok, tok), jnp.bfloat16), 1)
@@ -191,16 +192,16 @@
     return lax.optimization_barrier([tuple(table[m] for table in made) for m in range(micro)])
 
 
-def blocks_per_step(nblk):
-    return 8 if nblk % 8 == 0 else nblk
-
-
-def run_experts(made, tokens, weights, prev):
+def blocks_per_step(nblk, tok):
+    span = 2048 // tok
+    return span if nblk % span == 0 else nblk
+
+
+def run_experts(made, tokens, weights, prev, cap):
     seg, last_row, tiles, pos, cols = made
     experts, nblk, tok = pos.shape
     model, ff = weights[0].shape[1], weights[1].shape[1]
-    cap = tok // 2
-    span = blocks_per_step(nblk)
+    span = blocks_per_step(nblk, tok)
     rows = nblk * tok
     f32, bf16 = jnp.float32, jnp.bfloat16
     packed = span * cap + TILE
@@ -243,24 +244,30 @@
     def moe_layer(x, route_idx, gates, w_gate, w_up, w_down, grad_y):
         micro, tok = x.shape[0], x.shape[1]
         local = w_gate.shape[0]
-        gathered = [lax.all_gather(jnp.stack([x[m], grad_y[m]]), GROUP_AXES, axis=1, tiled=True) for m in range(micro)]
+        cap, half = tok // 2, tok // HALVES
+        pieces = [(m, slice(h * half, (h + 1) * half)) for m in range(micro) for h in range(HALVES)]
+        gathered = [lax.all_gather(jnp.stack([x[m, part], grad_y[m, part]]), GROUP_AXES, axis=1, tiled=True) for m, part in pieces]
         route_t = jnp.transpose(route_idx, (0, 2, 1))
         gates_t = jnp.transpose(gates, (0, 2, 1))
         hits = route_t[:, :, None, :] == jnp.arange(group_size * local)[None, None, :, None]
         table = jnp.where(jnp.any(hits, axis=1), jnp.sum(jnp.where(hits, gates_t[:, :, None, :], 0.0), axis=1), -1.0)
-        made = tables(lax.all_to_all(table.reshape(micro, group_size, local, tok), GROUP_AXES, 1, 1, tiled=True))
+        table = lax.all_to_all(table.reshape(micro, group_size, local, tok), GROUP_AXES, 1, 1, tiled=True)
+        table = jnp.moveaxis(table.reshape(micro, group_size, local, HALVES, half), 3, 1)
+        made = tables(table.reshape(micro * HALVES, group_size, local, half))
         weights = (jnp.concatenate([w_gate, w_up], axis=2), w_down, jnp.transpose(w_down, (0, 2, 1)),
                    jnp.concatenate([jnp.transpose(w_gate, (0, 2, 1)), jnp.transpose(w_up, (0, 2, 1))], axis=1))
-        outs_y, outs_dx, outs_dg = [], [], []
+        outs, gate_parts = [], []
         sums = None
-        for m in range(micro):
-            part, part_dg, *sums = run_experts(made[m], gathered[m], weights, sums)
-            whole = lax.psum_scatter(part, GROUP_AXES, scatter_dimension=0, tiled=True).astype(x.dtype)
-            outs_y.append(whole[:, :x.shape[2]])
-            outs_dx.append(whole[:, x.shape[2]:])
-            part_dg = jnp.transpose(part_dg[:, :local].reshape(group_size, tok, local), (0, 2, 1))
-            by_expert = lax.all_to_all(part_dg, GROUP_AXES, 0, 0, tiled=True).reshape(group_size * local, tok)
-            outs_dg.append(jnp.sum(jnp.where(hits[m], by_expert[None], 0.0), axis=1).T)
-        return (jnp.stack(outs_y), jnp.stack(outs_dx), jnp.stack(outs_dg), *sums)
+        for piece in range(len(pieces)):
+            part, part_dg, *sums = run_experts(made[piece], gathered[piece], weights, sums, cap)
+            outs.append(lax.psum_scatter(part, GROUP_AXES, scatter_dimension=0, tiled=True).astype(x.dtype))
+            gate_parts.append(part_dg[:, :local].reshape(group_size, half, local))
+        both = jnp.stack(outs).reshape(micro, tok, 2 * x.shape[2])
+        gate_parts = jnp.stack(gate_parts).reshape(micro, HALVES, group_size, half, local)
+        gate_parts = jnp.transpose(gate_parts, (2, 0, 4, 1, 3)).reshape(group_size, micro, local, tok)
+        by_expert = lax.all_to_all(gate_parts, GROUP_AXES, 0, 0, tiled=True)
+        by_expert = jnp.swapaxes(by_expert, 0, 1).reshape(micro, 1, group_size * local, tok)
+        grad_gates = jnp.transpose(jnp.sum(jnp.where(hits, by_expert, 0.0), axis=2), (0, 2, 1))
+        return (both[:, :, :x.shape[2]], both[:, :, x.shape[2]:], grad_gates, *sums)
 
     return jax.shard_map(moe_layer, mesh=mesh, in_specs=(tok_spec, tok_spec, tok_spec, w_spec, w_spec, w_spec, tok_spec), out_specs=(tok_spec, tok_spec, tok_spec, w_spec, w_spec, w_spec), check_vma=False)

time: 769 us -> 875 us (1.14)
  blocking collectives: 0 us -> 103 us
  Pallas kernels: 218 us -> 304 us
  starting transfers between devices: 85.2 us -> 10.1 us
  waiting for transfers between devices: 396 us -> 383 us
    all_to_all x0 -> x1, blocking collectives: none -> 103 us  [moe_layer(): by_expert = lax.all_to_all(gate_parts, GROUP_AXES, 0, 0, tiled=True)]
    pallas_call x2 -> x4, Pallas kernels: 218 us -> 304 us  [run_experts(): pl.pallas_call(functools.partial(expert_kernel, dims, first), name='exper...]
    all_to_all x2 -> x0, starting transfers between devices: 75.6 us -> none  [moe_layer(): lax.all_to_all(part_dg, GROUP_AXES, 0, 0, tiled=True)]
    all_gather x2 -> x4, waiting for transfers between devices: 54.3 us -> 17.3 us  [moe_layer(): lax.all_gather(jnp.stack([x[m, part], grad_y[m, part]]), GROUP_AXES, axis...]
    reduce_scatter x2 -> x4, waiting for transfers between devices: 330 us -> 365 us  [moe_layer(): lax.psum_scatter(part, GROUP_AXES, scatter_dimension=0, tiled=True)]
    all_to_all x2 -> x0, waiting for transfers between devices: 11.7 us -> none  [moe_layer(): lax.all_to_all(part_dg, GROUP_AXES, 0, 0, tiled=True)]
  transfers between devices with their start and end apart: 7 -> 9, of which waited for: 5 -> 4; matrix products, arithmetic and copies ran while one was open for 6% -> 6% of each run, Pallas kernels for 28% -> 35%
where the time goes in v2:
time: 875 us; the launch traced here: 874 us
  waiting for transfers between devices  383 us (44%)
  Pallas kernels  304 us (35%)
  blocking collectives  103 us (12%)
  local copies, waits for them, and re-layouts  45.5 us (5%)
  between operations  14.5 us (2%)
  other arithmetic  13.8 us (2%)
  starting transfers between devices  10.1 us (1%)
    reduce_scatter x4, waiting for transfers between devices, moe_layer(): lax.psum_scatter(part, GROUP_AXES, scatter_dimension=0, tiled=True)  365 us
    pallas_call x4, Pallas kernels, run_experts(): pl.pallas_call(functools.partial(expert_kernel, dims, first), name='exper...  304 us
    all_to_all x1, blocking collectives, moe_layer(): by_expert = lax.all_to_all(gate_parts, GROUP_AXES, 0, 0, tiled=True)  103 us
  transfers between devices with their start and end apart: 9, of which 4 were waited for; matrix products, arithmetic and copies ran while one was open for 6% of the time, Pallas kernels for 35%

profile of v2, /device:TPU:97, one launch (start us, length us, event | category | flops | bytes accessed | tf_op | source)
XLA Modules:
  0.0 874.0 jit_solution(11672961547066048691)
XLA Ops:
  7.2 0.1 all-gather.5.cloned.1.call-start
  7.3 1.7 fusion.16
  9.0 0.8 pad_maximum_fusion.2
  9.9 0.1 all-gather.7.cloned.1.call-start
  10.0 0.8 pad_maximum_fusion.3
  10.8 0.1 all-gather.9.cloned.1.call-start
  10.9 0.8 pad_maximum_fusion.4
  11.8 0.1 all-gather.11.cloned.1.call-start
  11.9 0.8 pad_maximum_fusion.5
  12.8 0.2 fusion.4
  12.9 0.1 select_reduce_fusion.1
  13.1 0.1 copy.95
  13.2 0.7 copy.96
  13.9 9.1 %all-to-all-start = ((f32[2,32,2,256]{3,2,0,1:T(2,128)}), f32[2,32,2,256]{3,2,0,1:T(2,128)S(1)}, u32[]{:S(2)}, u32[]{:S(2)}) async-start(f32[2,32,2,256]{3,2,0,1:T(2,128)} %copy.96), calls=%async_computation | async-start | bytes 262144 | tf_op jit(solution)/shard_map/all_to_all | solution.py:254
  23.1 0.1 reduce-scatter.5.cloned.1.call-start
  23.1 3.2 copy.106
  26.3 4.3 copy.107
  30.6 4.3 copy.105
  34.9 3.6 constant_dynamic-update-slice_fusion.1
  38.5 2.5 pad_maximum_fusion.refs_9_
  40.9 1.7 constant_dynamic-update-slice_fusion.refs_6_
  42.8 0.2 convert_reduce_fusion
  43.0 0.1 add.32
  43.1 1.5 reduce_window_sum.11
  44.6 0.1 slice.164
  44.8 0.6 squeeze.76.refs_0_
  45.4 0.6 squeeze.71.refs_0_
  46.0 0.7 squeeze.66.refs_0_
  46.7 0.6 squeeze.61.refs_0_
  47.3 0.1 copy.121
  47.4 0.2 fusion.20
  47.6 4.7 copy.104
  52.3 0.9 slice_reduce_fusion.1
  53.2 0.9 slice_reduce_fusion
  54.1 0.6 slice_bitcast_fusion
  54.7 6.8 fusion.3
  61.6 17.2 %all-gather.5.cloned.1.call-done.refs_4_ = bf16[2,4096,896]{2,1,0:T(8,128)(2,1)} async-done(((bf16[2,128,896]{2,1,0:T(8,128)(2,1)}), bf16[2,4096,896]{2,1,0:T(8,128)(2,1)}) %all-gather.5.cloned.1.call-update) | async-done | bytes 14680080 | tf_op jit(solution)/shard_map/all_gather | solution.py:249
  78.8 75.6 %experts_first.1 = (f32[4096,1792]{1,0:T(8,128)}, f32[4096,128]{1,0:T(8,128)}, f32[2,896,640]{2,1,0:T(8,128)}, f32[2,896,640]{2,1,0:T(8,128)}, f32[2,640,896]{2,1,0:T(8,128)}) custom-call(s32[2,32]{1,0:T(2,128)} %squeeze.61.refs_0_, s32[2,2]{1,0:T(2,128)} %get-tuple-element.47.refs_1_, s32[2,2]{1,0:T(2,128)} %get-tuple-element.48.refs_2_, ...), custom_call_target="tpu_custom_call" | custom-call | flops 42278584320 | bytes 44040192 | tf_op jit(solution)/shard_map/experts_first/pallas_call | solution.py:213
  154.3 0.1 reduce-scatter.5.cloned.1.call-update
  154.4 0.2 reduce-scatter.7.cloned.1.call-start
  154.7 78.6 %experts_next.3 = (f32[4096,1792]{1,0:T(8,128)}, f32[4096,128]{1,0:T(8,128)}, f32[2,896,640]{2,1,0:T(8,128)}, f32[2,896,640]{2,1,0:T(8,128)}, f32[2,640,896]{2,1,0:T(8,128)}) custom-call(s32[2,32]{1,0:T(2,128)} %squeeze.66.refs_0_, s32[2,2]{1,0:T(2,128)} %get-tuple-element.53.refs_1_, s32[2,2]{1,0:T(2,128)} %get-tuple-element.54.refs_2_, ...), custom_call_target="tpu_custom_call" | custom-call | flops 42278584320 | bytes 44040192 | tf_op jit(solution)/shard_map/experts_next/pallas_call | solution.py:213
  233.4 0.1 reduce-scatter.9.cloned.1.call-start
  233.5 75.1 %experts_next.4 = (f32[4096,1792]{1,0:T(8,128)}, f32[4096,128]{1,0:T(8,128)}, f32[2,896,640]{2,1,0:T(8,128)}, f32[2,896,640]{2,1,0:T(8,128)}, f32[2,640,896]{2,1,0:T(8,128)}) custom-call(s32[2,32]{1,0:T(2,128)} %squeeze.71.refs_0_, s32[2,2]{1,0:T(2,128)} %get-tuple-element.62.refs_1_, s32[2,2]{1,0:T(2,128)} %get-tuple-element.63.refs_2_, ...), custom_call_target="tpu_custom_call" | custom-call | flops 42278584320 | bytes 44040192 | tf_op jit(solution)/shard_map/experts_next/pallas_call | solution.py:213
  308.6 0.3 reduce-scatter.11.cloned.1.call-start
  308.9 75.2 %experts_next.5 = (f32[4096,1792]{1,0:T(8,128)}, f32[4096,128]{1,0:T(8,128)}, f32[2,896,640]{2,1,0:T(8,128)}, f32[2,896,640]{2,1,0:T(8,128)}, f32[2,640,896]{2,1,0:T(8,128)}) custom-call(s32[2,32]{1,0:T(2,128)} %squeeze.76.refs_0_, s32[2,2]{1,0:T(2,128)} %get-tuple-element.71.refs_1_, s32[2,2]{1,0:T(2,128)} %get-tuple-element.72.refs_2_, ...), custom_call_target="tpu_custom_call" | custom-call | flops 42278584320 | bytes 44040192 | tf_op jit(solution)/shard_map/experts_next/pallas_call | solution.py:213
  384.1 1.5 copy-done.2
  385.7 0.6 copy.108
  386.3 2.4 copy.109
  388.6 2.2 copy.110
  390.9 0.6 copy.111
  391.5 0.1 copy.117
  391.6 0.2 reshape.67
  391.8 102.9 %all_to_all.10 = f32[32,2,2,256]{3,2,1,0:T(2,128)S(1)} all-to-all(f32[32,2,2,256]{3,2,1,0:T(2,128)S(1)} %reshape.67), channel_id=1, replica_groups=mesh['rep'=1,'row'=4,'col'=4,'core'=2] {'row','col','core'}, dimensions={0} | all-to-all | bytes 262144 | tf_op jit(solution)/shard_map/all_to_all | solution.py:268
  494.7 0.1 copy.114
  494.8 0.7 select_reduce_fusion
  495.6 1.2 convert_bitcast_fusion.3
  496.8 71.4 %reduce-scatter.7.cloned.1.call-done = f32[128,1792]{1,0:T(8,128)} async-done(((f32[4096,1792]{1,0:T(8,128)}), f32[128,1792]{1,0:T(8,128)}) %reduce-scatter.7.cloned.1.call-update) | async-done | bytes 917520 | tf_op jit(solution)/shard_map/reduce_scatter | solution.py:263
  568.2 1.2 convert_bitcast_fusion.2
  569.4 146.9 %reduce-scatter.9.cloned.1.call-done = f32[128,1792]{1,0:T(8,128)} async-done(((f32[4096,1792]{1,0:T(8,128)}), f32[128,1792]{1,0:T(8,128)}) %reduce-scatter.9.cloned.1.call-update) | async-done | bytes 917520 | tf_op jit(solution)/shard_map/reduce_scatter | solution.py:263
  716.2 1.2 convert_bitcast_fusion.1
  717.5 146.9 %reduce-scatter.11.cloned.1.call-done = f32[128,1792]{1,0:T(8,128)} async-done(((f32[4096,1792]{1,0:T(8,128)}), f32[128,1792]{1,0:T(8,128)}) %reduce-scatter.11.cloned.1.call-update) | async-done | bytes 917520 | tf_op jit(solution)/shard_map/reduce_scatter | solution.py:263
  864.3 1.2 convert_bitcast_fusion
  865.6 0.2 pad_maximum_fusion.1
  865.8 1.4 fusion.15
  (42 shorter events, 0.7 us)
Async XLA Ops:
  7.2 5.6 copy-start.4
  7.2 5.7 copy-start.6
  7.2 71.6 %all-gather.5.cloned.1.call-start = ((), (), s32[]{:S(2)}) async-start(), calls=%async_computation.6 | async-start | bytes 15138816 | tf_op jit(solution)/shard_map/all_gather | solution.py:249
  9.9 144.8 %all-gather.7.cloned.1.call-start = ((), (), s32[]{:S(2)}) async-start(), calls=%async_computation.8 | async-start | bytes 15138816 | tf_op jit(solution)/shard_map/all_gather | solution.py:249
  10.8 222.6 %all-gather.9.cloned.1.call-start = ((), (), s32[]{:S(2)}) async-start(), calls=%async_computation.10 | async-start | bytes 15138816 | tf_op jit(solution)/shard_map/all_gather | solution.py:249
  11.8 297.1 %all-gather.11.cloned.1.call-start = ((), (), s32[]{:S(2)}) async-start(), calls=%async_computation.12 | async-start | bytes 15138816 | tf_op jit(solution)/shard_map/all_gather | solution.py:249
  13.9 28.7 %all-to-all-start = ((f32[2,32,2,256]{3,2,0,1:T(2,128)}), f32[2,32,2,256]{3,2,0,1:T(2,128)S(1)}, u32[]{:S(2)}, u32[]{:S(2)}) async-start(f32[2,32,2,256]{3,2,0,1:T(2,128)} %copy.96), calls=%async_computation | async-start | bytes 262144 | tf_op jit(solution)/shard_map/all_to_all | solution.py:254
  23.1 472.5 %reduce-scatter.5.cloned.1.call-start = ((), (), s32[]{:S(2)}) async-start(), calls=%async_computation.7 | async-start | bytes 30277632 | tf_op jit(solution)/shard_map/reduce_scatter | solution.py:263
  34.9 3.6 copy-start
  38.5 2.5 copy-start.1
  154.4 413.8 %reduce-scatter.7.cloned.1.call-start = ((), (), s32[]{:S(2)}) async-start(), calls=%async_computation.9 | async-start | bytes 30277632 | tf_op jit(solution)/shard_map/reduce_scatter | solution.py:263
  233.4 482.9 %reduce-scatter.9.cloned.1.call-start = ((), (), s32[]{:S(2)}) async-start(), calls=%async_computation.11 | async-start | bytes 30277632 | tf_op jit(solution)/shard_map/reduce_scatter | solution.py:263
  308.6 555.7 %reduce-scatter.11.cloned.1.call-start = ((), (), s32[]{:S(2)}) async-start(), calls=%async_computation.13 | async-start | bytes 30277632 | tf_op jit(solution)/shard_map/reduce_scatter | solution.py:263
  384.1 1.6 copy-start.2
  385.7 109.2 %copy-start.5 = (s32[2,256,8]{1,2,0:T(8,128)S(1)}, s32[2,256,8]{1,2,0:T(8,128)}, u32[]{:S(2)}) copy-start(s32[2,256,8]{1,2,0:T(8,128)} %param.8) | copy-start | bytes 49156
  386.3 4.6 copy-start.3
Sparse Core Ops, SparseCore 0:
  10.7 68.0 all-gather.4
  80.9 61.8 all-gather.6
  145.4 61.7 all-gather.8
  209.8 61.8 all-gather.10
  275.3 143.4 reduce-scatter.4
  422.5 145.6 reduce-scatter.6
  571.9 144.2 reduce-scatter.8
  720.0 144.2 reduce-scatter.10
